TPU v7x, 32 devices: a whole 2x2x4 slice. The times are simulated.
32 devices in a mesh: grp: 4 (over y, core), dev: 8 (over z, x).
Axes of the slice: x: 2, y: 2, z: 4, core: 2. Of those that a mesh axis runs over, the one named last changes fastest.
Arguments:
- targets: float32 [64, 16384], P(None, ('grp', 'dev')), may hold values from -1.7 to 1.7
- source_grid: int32 [64, 4096], P(None, ('grp', 'dev')), may hold values from -1331000 to 1331000
- source_weight: int32 [1, 4096], P(None, ('grp', 'dev')), may hold values from 1 to 1024
Outputs:
- kernel_sum: float32 [16384], P(('grp', 'dev'))
All inputs are finite; a program needn't handle non-finite values.
Results may differ from a plain program's by a relative error of at most 0.00017.
Values sent between devices are 32-bit elements; how exact they have to be, the bound alone decides.
A program may use at most 64 MiB of HBM per device.

v0:
```python
import functools
import math

import jax
import jax.numpy as jnp
from jax import lax
from jax.experimental import pallas as pl
from jax.experimental.pallas import tpu as pltpu
from jax.sharding import PartitionSpec as P

KERNEL_RATE = 0.7
RATE = KERNEL_RATE * math.log2(math.e)
GRID_SCALE = 1.0 / 1048576.0
WEIGHT_SCALE = 1.0 / 16.0
EXTRA = 16
LANES = 128
MESH = pl.DeviceIdType.MESH


def slot_of(layer, rx, ry):
    return layer * 4 + rx * 2 + ry


def three_parts(value):
    first = value.astype(jnp.bfloat16).astype(jnp.float32)
    rest = value - first
    second = rest.astype(jnp.bfloat16).astype(jnp.float32)
    return first, second, rest - second


def extra_rows(rows, norm, norm_at, ones_at):
    row = lax.broadcasted_iota(jnp.int32, (rows, norm.shape[1]), 0)
    result = jnp.where((row >= ones_at) & (row < ones_at + 3), 1.0, 0.0)
    for i, part in enumerate(three_parts(norm)):
        result = jnp.where(row == norm_at + i, part, result)
    return result


def kernel(
    layers, tgt_hbm, grid_hbm, weight_hbm, out_ref, tgt, slots, lhs, acc, swap, local_sem, send_sem, recv_sem, swap_sem
):
    _, depth, count = tgt.shape
    me_grp, me_dev = lax.axis_index("grp"), lax.axis_index("dev")
    my_y, my_core = me_grp // 2, me_grp % 2
    my_z, my_x = me_dev // 2, me_dev % 2
    along_x = {"grp": me_grp, "dev": my_z * 2 + (1 - my_x)}
    along_y = {"grp": (1 - my_y) * 2 + my_core, "dev": me_dev}
    diagonal = {"grp": (1 - my_y) * 2 + my_core, "dev": my_z * 2 + (1 - my_x)}
    diagonal = {"grp": (1 - my_y) * 2 + my_core, "dev": my_z * 2 + (1 - my_x)}
    across = {"grp": my_y * 2 + (1 - my_core), "dev": me_dev}

    below, above = my_z, layers - 1 - my_z
    both = jnp.minimum(below, above)

    def along_z(step):
        return {"grp": me_grp, "dev": ((my_z + step) % layers) * 2 + my_x}

    def origin(j):
        alternate = my_z + ((j + 1) // 2) * (1 if j % 2 else -1)
        onward = jnp.where(above > below, my_z + (j - both), my_z - (j - both))
        return jnp.where(j <= 2 * both, alternate, onward)

    own = [
        pltpu.make_async_copy(grid_hbm, slots.at[4 * my_z, pl.ds(0, depth)], local_sem.at[0]),
        pltpu.make_async_copy(weight_hbm, slots.at[4 * my_z, pl.ds(depth, 1)], local_sem.at[1]),
    ]
    targets_in = pltpu.make_async_copy(tgt_hbm, tgt.at[0], local_sem.at[2])
    for copy in own:
        copy.start()
    targets_in.start()

    barrier = pltpu.get_barrier_semaphore()
    partners = [along_z(step) for step in range(1, layers)] + [along_x, along_y, diagonal, across]
    for partner in partners:
        pl.semaphore_signal(barrier, inc=1, device_id=partner, device_id_type=MESH)
    pl.semaphore_wait(barrier, len(partners))
    for copy in own:
        copy.wait()

    sent = []

    def view(slot):
        return slots.at[slot, pl.ds(0, depth + 1)]

    def send(source, target, device):
        copy = pltpu.make_async_remote_copy(
            src_ref=view(source),
            dst_ref=view(target),
            send_sem=send_sem.at[len(sent)],
            recv_sem=recv_sem.at[target],
            device_id=device,
            device_id_type=MESH,
        )
        copy.start()
        sent.append(copy)

    def arrive(slot):
        pltpu.make_async_copy(view(slot), view(slot), recv_sem.at[slot]).wait()

    layer = [origin(j) for j in range(layers)]
    mine = slot_of(layer[0], 0, 0)
    for step in range(1, layers):
        send(mine, mine, along_z(step))
    send(mine, mine + 2, along_x)
    send(mine, mine + 1, along_y)

    def swap_copy(source, target, i):
        return pltpu.make_async_remote_copy(
            src_ref=source,
            dst_ref=target,
            send_sem=swap_sem.at[2 * i],
            recv_sem=swap_sem.at[2 * i + 1],
            device_id=across,
            device_id_type=MESH,
        )

    targets_in.wait()
    swap_targets = swap_copy(tgt.at[0], tgt.at[1], 0)
    swap_targets.start()
    tail = jnp.zeros((2 * depth - EXTRA, count), jnp.float32)
    for which in range(2):
        if which == 1:
            swap_targets.wait()
        t = tgt[which]
        norm = jnp.sum(t * t, axis=0, keepdims=True) * (-RATE)
        t1, t2, t3 = three_parts(t * (2.0 * RATE))
        ext = extra_rows(EXTRA, norm, 0, 3)
        for i, pair in enumerate(((t1, t2), (t3, t1), (t2, t1), (ext, tail))):
            block = jnp.concatenate(pair, axis=0)
            lhs[which, :, 2 * depth * i : 2 * depth * (i + 1)] = block.T.astype(jnp.bfloat16)
    acc[...] = jnp.zeros_like(acc)

    def forward(j, rx, ry):
        slot = slot_of(layer[j], rx, ry)
        arrive(slot)
        if rx == 0 and ry == 0:
            send(slot, slot + 2, along_x)
            send(slot, slot + 1, along_y)
            if j > 0:
                send(slot, slot + 3, diagonal)
        elif j > 0:
            pass
        elif rx == 1 and ry == 0 and j % 2 == 0:
            send(slot, slot + 1, along_y)
        elif rx == 0 and ry == 1 and j % 2 == 1:
            send(slot, slot + 2, along_x)

    def source_side(pair):
        blocks = jnp.concatenate([slots[slot_of(layer[j], rx, ry)] for j, rx, ry in pair], axis=1)
        p = blocks[:depth].astype(jnp.float32) * GRID_SCALE
        mass = blocks[depth : depth + 1].astype(jnp.float32) * WEIGHT_SCALE
        p_norm = jnp.sum(p * p, axis=0, keepdims=True) * (-RATE)
        p1, p2, p3 = three_parts(p)
        p_ext = extra_rows(EXTRA, p_norm, 3, 0)
        p_tail = jnp.zeros((2 * depth - EXTRA, p.shape[1]), jnp.float32)
        return jnp.concatenate([p1, p1, p1, p2, p2, p3, p_ext, p_tail], axis=0).astype(jnp.bfloat16), mass

    def add_terms(which, rhs, mass):
        terms = jnp.exp2(jnp.dot(lhs[which], rhs, preferred_element_type=jnp.float32)) * mass
        total = acc[which]
        for i in range(terms.shape[1] // LANES):
            total = total + terms[:, i * LANES : (i + 1) * LANES]
        acc[which] = total

    def compute(pair):
        side = source_side(pair)
        add_terms(1, *side)
        add_terms(0, *side)

    def reduced(which):
        return jnp.sum(acc[which].T, axis=0, keepdims=True)

    far = range(1, layers)
    forward(1, 0, 0)
    forward(0, 1, 0)
    forward(0, 0, 1)
    for j in far[1:]:
        forward(j, 0, 0)
    forward(0, 1, 1)
    ready = [(0, 0, 0), (0, 1, 0), (0, 0, 1)] + [(j, 0, 0) for j in far] + [(0, 1, 1)]
    for j in far:
        forward(j, 1, 0)
        forward(j, 0, 1)
        ready += [(j, 1, 0), (j, 0, 1)]
        for _ in range(min(2, len(ready) // 2)):
            compute(ready[:2])
            ready = ready[2:]
    for j in far:
        while len(ready) > 1:
            compute(ready[:2])
            ready = ready[2:]
        forward(j, 1, 1)
        ready += [(j, 1, 1)]
    while len(ready) > 2:
        compute(ready[:2])
        ready = ready[2:]
    side = source_side(ready)
    add_terms(1, *side)
    swap[0] = reduced(1)
    for copy in sent:
        copy.wait_send()
    swap_sums = swap_copy(swap.at[0], swap.at[1], 1)
    swap_sums.start()
    add_terms(0, *side)
    result = reduced(0)
    swap_sums.wait()
    out_ref[...] = result + swap[1]

def shards(layers, targets, source_grid, source_weight):
    depth, count = targets.shape
    width = source_grid.shape[1]
    slot_count = layers * 4
    copies = slot_count
    result = pl.pallas_call(
        functools.partial(kernel, layers),
        out_shape=jax.ShapeDtypeStruct((1, count), jnp.float32),
        in_specs=[pl.BlockSpec(memory_space=pltpu.HBM)] * 3,
        out_specs=pl.BlockSpec(memory_space=pltpu.VMEM),
        scratch_shapes=[
            pltpu.VMEM((2, depth, count), jnp.float32),
            pltpu.VMEM((slot_count, depth + 8, width), jnp.int32),
            pltpu.VMEM((2, count, 8 * depth), jnp.bfloat16),
            pltpu.VMEM((2, count, LANES), jnp.float32),
            pltpu.VMEM((2, 1, count), jnp.float32),
            pltpu.SemaphoreType.DMA((3,)),
            pltpu.SemaphoreType.DMA((copies,)),
            pltpu.SemaphoreType.DMA((slot_count,)),
            pltpu.SemaphoreType.DMA((4,)),
        ],
        compiler_params=pltpu.CompilerParams(collective_id=0, has_side_effects=True, vmem_limit_bytes=67043328),
    )(targets, source_grid, source_weight)
    return result.reshape(count)


def solution(mesh):
    layers = mesh.shape["dev"] // 2
    in_specs = (P(None, ("grp", "dev")), P(None, ("grp", "dev")), P(None, ("grp", "dev")))
    out_specs = P(("grp", "dev"))
    return jax.shard_map(
        functools.partial(shards, layers), mesh=mesh, in_specs=in_specs, out_specs=out_specs, check_vma=False
    )
```

profile of v0, /device:TPU:3, one launch (start us, length us, event | category | flops | bytes accessed | tf_op | source)
XLA Modules:
  0.0 18.9 jit_solution(1819573656164129436)
XLA Ops:
  0.0 17.6 %shard_map.37 = f32[1,512]{1,0:T(1,128)} custom-call(f32[64,512]{1,0:T(8,128)} %tgt_hbm.1, s32[64,128]{1,0:T(8,128)} %grid_hbm.1, s32[1,128]{1,0:T(1,128)} %weight_hbm.1), custom_call_target="tpu_custom_call" | custom-call | tf_op jit(solution)/shard_map/pallas_call | solution.py:214
  17.6 1.3 %copy.5 = f32[512]{0:T(512)} copy(f32[512]{0:T(512)} %bitcast.1) | data formatting | bytes 4096
where the time goes:
time: 19 us; the launch traced here: 18.9 us
  Pallas kernels  17.6 us (93%)
  local copies, waits for them, and re-layouts  1.26 us (7%)
    pallas_call x1, Pallas kernels, shards(): pl.pallas_call(functools.partial(kernel, layers), out_shape=jax.ShapeDtyp...  17.6 us
    unnamed x1, local copies, waits for them, and re-layouts  1.26 us

commit v1 on v0

--- a/solution.py
+++ b/solution.py
@@ -13,6 +13,7 @@
 GRID_SCALE = 1.0 / 1048576.0
 WEIGHT_SCALE = 1.0 / 16.0
 EXTRA = 16
+VMEM_GRANT = 32 * 1024 * 1024
 LANES = 128
 MESH = pl.DeviceIdType.MESH
 
@@ -227,8 +228,8 @@
             pltpu.SemaphoreType.DMA((slot_count,)),
             pltpu.SemaphoreType.DMA((4,)),
         ],
-        compiler_params=pltpu.CompilerParams(collective_id=0, has_side_effects=True, vmem_limit_bytes=67043328),
-    )(targets, source_grid, source_weight)
+        compiler_params=pltpu.CompilerParams(collective_id=0, has_side_effects=True, vmem_limit_bytes=VMEM_GRANT),
+    )(*[pltpu.with_memory_space_constraint(a, pltpu.HBM) for a in (targets, source_grid, source_weight)])
     return result.reshape(count)
 
 

time: 19 us -> 17.8 us (0.937)
  local copies, waits for them, and re-layouts: 1.26 us -> 0.58 us
  Pallas kernels: 17.6 us -> 17 us
    unnamed x1, local copies, waits for them, and re-layouts: 1.26 us -> 0.58 us
    pallas_call x1, Pallas kernels: 17.6 us -> 17 us  [shards(): pl.pallas_call(functools.partial(kernel, layers), out_shape=jax.ShapeDtyp...]
where the time goes in v1:
time: 17.8 us; the launch traced here: 17.6 us
  Pallas kernels  17 us (96%)
  local copies, waits for them, and re-layouts  0.58 us (3%)
    pallas_call x1, Pallas kernels, shards(): pl.pallas_call(functools.partial(kernel, layers), out_shape=jax.ShapeDtyp...  17 us
    unnamed x1, local copies, waits for them, and re-layouts  0.58 us

profile of v1, /device:TPU:3, one launch (start us, length us, event | category | flops | bytes accessed | tf_op | source)
XLA Modules:
  0.0 17.6 jit_solution(2895930710249235123)
XLA Ops:
  0.0 17.0 %shard_map.37 = f32[1,512]{1,0:T(1,128)S(1)} custom-call(f32[64,512]{1,0:T(8,128)} %tgt_hbm.1, s32[64,128]{1,0:T(8,128)} %grid_hbm.1, s32[1,128]{1,0:T(1,128)} %weight_hbm.1), custom_call_target="tpu_custom_call" | custom-call | tf_op jit(solution)/shard_map/pallas_call | solution.py:215
  17.0 0.6 %copy.5 = f32[512]{0:T(512)} copy(f32[512]{0:T(512)S(1)} %bitcast.1) | data formatting | bytes 4096
